TPU v7x, 32 devices: a whole 2x2x4 slice. The times are simulated.
32 devices in a mesh: dp: 16 (over z, x, core), mp: 2 (over y).
Axes of the slice: x: 2, y: 2, z: 4, core: 2. Of those that a mesh axis runs over, the one named last changes fastest.
Arguments:
- tokens: bfloat16 [2560, 1024], P('dp', 'mp'), may hold values from -6 to 6
- slot_embed: bfloat16 [2560, 1024], P('dp', 'mp'), may hold values from -0.1875 to 0.1875
- price_units: int32 [2560], P('dp'), may hold values from 0 to 1535
- unassigned: int32 [2560], P('dp'), may hold values from 0 to 1, as said below
Outputs:
- new_prices: float32 [2560], P(('dp', 'mp'))
- margins: float32 [2560], P('dp')
- unassigned_count: int32 [], replicated
Inputs may be any that keep to these rules, and one draw needn't show every extreme that they name: At most 128 of the 160 tokens of each index of dp are unassigned, and some index of dp has exactly 128 in every draw.
All inputs are finite; a program needn't handle non-finite values.
Results may differ from a plain program's by a relative error of at most 0.0004.
Values may be sent and summed in bfloat16 or wider, within the bound.
A program may use at most 128 MiB of HBM per device.

v0:
```python
import jax
import jax.numpy as jnp
from jax import lax
from jax.sharding import PartitionSpec as P

BUSY = 128
unit_price = 1.0 / 512.0


def merged(x, axis, combine):
    everything = jax.tree.map(lambda part: lax.all_gather(part, axis), x)
    first = jax.tree.map(lambda part: part[0], everything)

    def turn(k, so_far):
        return combine(so_far, jax.tree.map(lambda part: part[k], everything))

    return lax.fori_loop(1, lax.axis_size(axis), turn, first)


def top_two(values):
    best_value = jnp.max(values, axis=1)
    where_best = jnp.argmax(values, axis=1)
    column_ids = lax.broadcasted_iota(jnp.int32, values.shape, 1)
    second_value = jnp.max(jnp.where(column_ids == where_best[:, None], -jnp.inf, values), axis=1)
    return (best_value, second_value)


def keep_two(first, later):
    best_first, second_first = first
    best_later, second_later = later
    best_value = jnp.maximum(best_first, best_later)
    second_value = jnp.maximum(
        jnp.minimum(best_first, best_later), jnp.maximum(second_first, second_later)
    )
    return (best_value, second_value)


def compact(mask, busy):
    length = mask.shape[0]
    positions = lax.broadcasted_iota(jnp.int32, (length,), 0)
    ordering = jnp.argsort(jnp.where(mask > 0, positions, positions + length))[:busy]
    return (ordering, mask[ordering] > 0)


def spread_back(ordering, is_valid, margin_rows, length):
    positions = lax.broadcasted_iota(jnp.int32, (ordering.shape[0], length), 1)
    hits = (positions == ordering[:, None]) & is_valid[:, None]
    return jnp.sum(jnp.where(hits, margin_rows[:, None], jnp.float32(0.0)), axis=0)


def excess_of(values, second_value, is_valid):
    excess = jnp.where(is_valid[:, None], values - second_value[:, None], -jnp.inf)
    return jnp.max(excess, axis=0)


def on_device(tokens, slot_embed, price_units, unassigned):
    dp_count = lax.axis_size("dp")
    mp_count = lax.axis_size("mp")
    mp_index = lax.axis_index("mp")
    slot_dev = slot_embed.shape[0]
    half = slot_dev // mp_count
    columns = dp_count * half
    ordering, is_valid = compact(unassigned, BUSY)
    bidders = tokens[ordering]
    own_units = lax.dynamic_slice_in_dim(price_units, mp_index * half, half)
    own_prices = own_units.astype(jnp.float32) * unit_price
    whole_bidders = lax.all_gather(bidders, "mp", axis=1, tiled=True)
    slot_rows_whole = lax.all_to_all(slot_embed, "mp", split_axis=0, concat_axis=1, tiled=True)
    unit_all = jnp.zeros((columns,), jnp.int32)
    slot_rows = lax.all_gather(slot_rows_whole, "dp", axis=0, tiled=True)
    unit_rows = lax.all_gather(own_units, "dp", axis=0, tiled=True)
    block = jnp.einsum("bd,sd->bs", whole_bidders, slot_rows, preferred_element_type=jnp.float32)
    unit_all = lax.dynamic_update_slice_in_dim(unit_all, unit_rows, jnp.int32(0), 0)
    scores, unit_all = (block, unit_all)
    values = scores - (unit_all.astype(jnp.float32) * unit_price)[None, :]
    best_value, second_value = merged(top_two(values), "mp", keep_two)
    terms = excess_of(values, second_value, is_valid).reshape(dp_count, half)
    owner_terms = lax.all_to_all(terms, "dp", split_axis=0, concat_axis=0, tiled=True)
    highest = jnp.max(owner_terms, axis=0)
    new_prices = own_prices + jnp.maximum(highest, jnp.float32(0.0))
    margin_rows = jnp.where(is_valid, best_value - second_value, jnp.float32(0.0))
    margins = spread_back(ordering, is_valid, margin_rows, unassigned.shape[0])
    bidder_total = lax.psum(jnp.sum(unassigned), "dp")
    return (new_prices, margins, bidder_total)


def solution(mesh):
    return jax.shard_map(
        on_device,
        mesh=mesh,
        in_specs=(P("dp", "mp"), P("dp", "mp"), P("dp"), P("dp")),
        out_specs=(P(("dp", "mp")), P("dp"), P()),
        check_vma=False,
    )
```

profile of v0, /device:TPU:0, one launch (start us, length us, event | category | flops | bytes accessed | tf_op | source)
XLA Modules:
  0.0 91.2 jit_solution(4303682870376259929)
XLA Ops:
  7.2 0.0 all-gather.7.cloned.1.call-start
  7.2 9.2 %all_to_all.28 = bf16[2,80,512]{2,1,0:T(8,128)(2,1)S(1)} all-to-all(bf16[2,80,512]{2,1,0:T(8,128)(2,1)} %bitcast.19), channel_id=1, replica_groups=mesh['dp'=16,'mp'=2] {'mp'}, dimensions={0} | all-to-all | bytes 327680 | tf_op jit(solution)/shard_map/all_to_all | solution.py:68
  16.4 0.7 copy.12
  17.1 0.0 all-gather.7.cloned.1.call-update
  17.1 1.3 %fusion.6 = (s32[]{:T(128)}, s32[160]{0:T(256)S(1)}) fusion(s32[160]{0:T(256)} %param.7), kind=kLoop, calls=%fused_computation.23 | loop fusion | flops 639 | bytes 1284 | tf_op jit(solution)/shard_map/reduce_sum | solution.py:83
  18.4 3.2 %sort.17 = (s32[160]{0:T(256)}, s32[160]{0:T(256)S(1)}) sort(s32[160]{0:T(256)S(1)} %get-tuple-element.35, s32[160]{0:T(256)S(1)} %iota.27), dimensions={0}, to_apply=%region_0.1 | sort | flops 1280 | bytes 2560 | tf_op jit(solution)/shard_map/jit(argsort)/sort | solution.py:41
  21.6 1.6 %gather_fusion = s32[128]{0:T(128)S(1)} fusion(s32[160]{0:T(256)} %param.7, s32[1024]{0:T(1024)S(1)} %pad_clamp_fusion), kind=kCustom, calls=%fused_computation | custom fusion | bytes 1536 | tf_op jit(solution)/shard_map/gather | solution.py:42
  23.3 0.8 gather_fusion.1
  24.1 1.2 %dynamic-slice = u32[1]{0:T(128)} dynamic-slice(u32[32]{0:T(128)} %constant.16, u32[]{:T(128)S(6)} %add.30), dynamic_slice_sizes={1} | dynamic-slice | bytes 12
  26.0 0.9 dynamic-slice_dynamic-update-slice_fusion
  26.9 13.7 %all-reduce.1 = (s32[1280]{0:T(1024)S(1)}, s32[]{:T(128)}) all-reduce(s32[1280]{0:T(1024)S(1)} %dynamic-slice_dynamic-update-slice_fusion, s32[]{:T(128)} %get-tuple-element.34), channel_id=1, replica_groups=mesh['dp'=16,'mp'=2] {'dp'}, use_global_device_ids=true, to_apply=%add | all-reduce | flops 1281 | bytes 10248
  40.6 5.6 %all-gather = bf16[128,1024]{1,0:T(8,128)(2,1)S(1)} all-gather(bf16[128,512]{1,0:T(8,128)(2,1)S(1)} %gather_fusion.1), channel_id=2, replica_groups=mesh['dp'=16,'mp'=2] {'mp'}, dimensions={1}, use_global_device_ids=true | all-gather | bytes 393216 | tf_op jit(solution)/shard_map/all_gather | solution.py:67
  46.3 14.8 %all-gather.7.cloned.1.call-done = bf16[1280,1024]{1,0:T(8,128)(2,1)} async-done(((bf16[80,1024]{1,0:T(8,128)(2,1)}), bf16[1280,1024]{1,0:T(8,128)(2,1)}) %all-gather.7.cloned.1.call-update) | async-done | bytes 2621456 | tf_op jit(solution)/shard_map/all_gather | solution.py:70
  61.0 2.7 %convolution_subtract_fusion = f32[128,1280]{1,0:T(8,128)S(1)} fusion(bf16[128,1024]{1,0:T(8,128)(2,1)S(1)} %all-gather, bf16[1280,1024]{1,0:T(8,128)(2,1)} %all-gather.7.cloned.1.call-done, f32[1280]{0:T(1024)S(1)} %convert_multiply_fusion), kind=kOutput, calls=%fused_computation.2 | convolution fusion | flops 335708160 | bytes 3544064 | tf_op jit(solution)/shard_map/bd,sd->bs/dot_general | solution.py:72
  63.8 0.4 iota_reduce_fusion
  64.2 4.2 %all-gather.3 = f32[2,1,128]{2,1,0:T(1,128)S(1)} all-gather(f32[1,1,128]{2,1,0:T(1,128)S(1)} %bitcast.21), channel_id=3, replica_groups=mesh['dp'=16,'mp'=2] {'mp'}, dimensions={0}, use_global_device_ids=true | all-gather | bytes 1536 | tf_op jit(solution)/shard_map/all_gather | solution.py:11
  68.4 0.2 select_reduce_fusion.1
  68.6 4.2 %all-gather.4 = f32[2,1,128]{2,1,0:T(1,128)S(1)} all-gather(f32[1,1,128]{2,1,0:T(1,128)S(1)} %bitcast.22), channel_id=4, replica_groups=mesh['dp'=16,'mp'=2] {'mp'}, dimensions={0}, use_global_device_ids=true | all-gather | bytes 1536 | tf_op jit(solution)/shard_map/all_gather | solution.py:11
  72.9 0.1 select_reduce_fusion
  73.0 0.7 all_to_all.24
  73.7 3.6 %all-to-all-start.1 = ((f32[16,1,80]{2,1,0:T(1,128)}), f32[16,1,80]{2,1,0:T(1,128)S(1)}, u32[]{:S(2)}, u32[]{:S(2)}) async-start(f32[16,1,80]{2,1,0:T(1,128)} %all_to_all.24), calls=%async_computation.1 | async-start | bytes 16384 | tf_op jit(solution)/shard_map/all_to_all | solution.py:78
  77.3 0.7 select_reduce_fusion.2
  77.9 5.8 %all-to-all-done.1 = f32[16,1,80]{2,1,0:T(1,128)S(1)} async-done(((f32[16,1,80]{2,1,0:T(1,128)}), f32[16,1,80]{2,1,0:T(1,128)S(1)}, u32[]{:S(2)}, u32[]{:S(2)}) %all-to-all-start.1) | async-done | bytes 5152 | tf_op jit(solution)/shard_map/all_to_all | solution.py:78
  83.7 0.6 maximum_add_fusion
  (12 shorter events, 0.1 us)
Async XLA Ops:
  7.2 16.1 %copy-start = (bf16[160,512]{1,0:T(8,128)(2,1)S(1)}, bf16[160,512]{1,0:T(8,128)(2,1)}, u32[]{:S(2)}) copy-start(bf16[160,512]{1,0:T(8,128)(2,1)} %param.4) | copy-start | bytes 491524
  7.2 53.9 %all-gather.7.cloned.1.call-start = ((), (), s32[]{:S(2)}) async-start(), calls=%async_computation.2 | async-start | bytes 2785280 | tf_op jit(solution)/shard_map/all_gather | solution.py:70
  46.2 37.5 %copy-start.1 = (s32[160]{0:T(256)S(1)}, s32[160]{0:T(256)}, u32[]{:S(2)}) copy-start(s32[160]{0:T(256)} %param.6) | copy-start | bytes 1924
  73.7 10.0 %all-to-all-start.1 = ((f32[16,1,80]{2,1,0:T(1,128)}), f32[16,1,80]{2,1,0:T(1,128)S(1)}, u32[]{:S(2)}, u32[]{:S(2)}) async-start(f32[16,1,80]{2,1,0:T(1,128)} %all_to_all.24), calls=%async_computation.1 | async-start | bytes 16384 | tf_op jit(solution)/shard_map/all_to_all | solution.py:78
Sparse Core Ops, SparseCore 0:
  17.2 43.7 all-gather.6
where the time goes:
time: 91.5 us; the launch traced here: 91.2 us
  blocking collectives  37 us (40%)
  waiting for transfers between devices  20.6 us (23%)
  between operations  14.7 us (16%)
  other arithmetic  6.56 us (7%)
  local copies, waits for them, and re-layouts  5.97 us (7%)
  starting transfers between devices  3.59 us (4%)
  matrix products  2.73 us (3%)
    all_gather x1, waiting for transfers between devices, on_device(): slot_rows = lax.all_gather(slot_rows_whole, 'dp', axis=0, tiled=True)  14.8 us
    unnamed x1, blocking collectives  13.7 us
    all_to_all x1, blocking collectives, on_device(): lax.all_to_all(slot_embed, 'mp', split_axis=0, concat_axis=1, tiled=True)  9.2 us
    all_gather x2, blocking collectives, merged(): everything = jax.tree.map(lambda part: lax.all_gather(part, axis), x)  8.47 us
    all_to_all x1, waiting for transfers between devices, on_device(): lax.all_to_all(terms, 'dp', split_axis=0, concat_axis=0, tiled=True)  5.75 us
    all_gather x1, blocking collectives, on_device(): whole_bidders = lax.all_gather(bidders, 'mp', axis=1, tiled=True)  5.62 us
    all_to_all x1, starting transfers between devices, on_device(): lax.all_to_all(terms, 'dp', split_axis=0, concat_axis=0, tiled=True)  3.55 us
    sort x1, other arithmetic, compact(): jnp.argsort(jnp.where(mask > 0, positions, positions + length))[:busy]  3.17 us
  transfers between devices with their start and end apart: 2, of which 2 were waited for; matrix products, arithmetic and copies ran while one was open for 11% of the time, Pallas kernels for 0%

commit v1 on v0

--- a/solution.py
+++ b/solution.py
@@ -5,6 +5,12 @@
 
 BUSY = 128
 unit_price = 1.0 / 512.0
+
+
+def joined_along(blocks, dim):
+    shape = list(blocks.shape[1:])
+    shape[dim] *= blocks.shape[0]
+    return jnp.moveaxis(blocks, 0, dim).reshape(shape)
 
 
 def merged(x, axis, combine):
@@ -67,9 +73,19 @@
     whole_bidders = lax.all_gather(bidders, "mp", axis=1, tiled=True)
     slot_rows_whole = lax.all_to_all(slot_embed, "mp", split_axis=0, concat_axis=1, tiled=True)
     unit_all = jnp.zeros((columns,), jnp.int32)
-    slot_rows = lax.all_gather(slot_rows_whole, "dp", axis=0, tiled=True)
     unit_rows = lax.all_gather(own_units, "dp", axis=0, tiled=True)
-    block = jnp.einsum("bd,sd->bs", whole_bidders, slot_rows, preferred_element_type=jnp.float32)
+    size, mine, width = (lax.axis_size("dp"), lax.axis_index("dp"), slot_rows_whole.shape[0])
+    ahead = [(i, (i + 1) % size) for i in range(size)]
+    pieces = []
+    block_2 = slot_rows_whole
+    for step in range(size):
+        coming = block_2 if step == size - 1 else lax.ppermute(block_2, "dp", ahead)
+        pieces.append(
+            jnp.einsum("bd,sd->bs", whole_bidders, block_2, preferred_element_type=jnp.float32)
+        )
+        block_2 = coming
+    pieces = jnp.stack(pieces)[(mine - jnp.arange(size)) % size]
+    block = joined_along(pieces, 1)
     unit_all = lax.dynamic_update_slice_in_dim(unit_all, unit_rows, jnp.int32(0), 0)
     scores, unit_all = (block, unit_all)
     values = scores - (unit_all.astype(jnp.float32) * unit_price)[None, :]

time: 91.5 us -> 168 us (1.84)
  waiting for transfers between devices: 20.6 us -> 114 us
  between operations: 14.7 us -> 1.55 us
  blocking collectives: 37 us -> 28 us
  starting transfers between devices: 3.59 us -> 7.99 us
    ppermute x0 -> x15, waiting for transfers between devices: none -> 108 us  [on_device(): coming = block_2 if step == size - 1 else lax.ppermute(block_2, 'dp', ahead)]
    all_gather x1 -> x0, waiting for transfers between devices: 14.8 us -> none  [on_device(): slot_rows = lax.all_gather(slot_rows_whole, 'dp', axis=0, tiled=True)]
    all_to_all x1 -> x0, blocking collectives: 9.2 us -> none  [on_device(): lax.all_to_all(slot_embed, 'mp', split_axis=0, concat_axis=1, tiled=True)]
    all_to_all x0 -> x1, starting transfers between devices: none -> 4.41 us  [on_device(): lax.all_to_all(slot_embed, 'mp', split_axis=0, concat_axis=1, tiled=True)]
    dot_general x1 -> x16, matrix products: 2.73 us -> 3.42 us  [on_device(): jnp.einsum('bd,sd->bs', whole_bidders, block_2, preferred_element_type=jn...]
  transfers between devices with their start and end apart: 2 -> 17, of which waited for: 2 -> 16; matrix products, arithmetic and copies ran while one was open for 11% -> 6% of each run, Pallas kernels for 0% -> 0%
where the time goes in v1:
time: 168 us
  waiting for transfers between devices  114 us (68%)
  blocking collectives  28 us (17%)
  starting transfers between devices  7.99 us (5%)
  other arithmetic  7.7 us (5%)
  local copies, waits for them, and re-layouts  5.53 us (3%)
  matrix products  3.42 us (2%)
    ppermute x15, waiting for transfers between devices, on_device(): coming = block_2 if step == size - 1 else lax.ppermute(block_2, 'dp', ahead)  108 us
    unnamed x1, blocking collectives  13.9 us
    all_gather x2, blocking collectives, merged(): everything = jax.tree.map(lambda part: lax.all_gather(part, axis), x)  8.46 us
    all_to_all x1, waiting for transfers between devices, on_device(): lax.all_to_all(terms, 'dp', split_axis=0, concat_axis=0, tiled=True)  5.72 us
    all_gather x1, blocking collectives, on_device(): whole_bidders = lax.all_gather(bidders, 'mp', axis=1, tiled=True)  5.63 us
    all_to_all x1, starting transfers between devices, on_device(): lax.all_to_all(slot_embed, 'mp', split_axis=0, concat_axis=1, tiled=True)  4.41 us
    all_to_all x1, starting transfers between devices, on_device(): lax.all_to_all(terms, 'dp', split_axis=0, concat_axis=0, tiled=True)  3.49 us
    dot_general x16, matrix products, on_device(): jnp.einsum('bd,sd->bs', whole_bidders, block_2, preferred_element_type=jn...  3.42 us
  transfers between devices with their start and end apart: 17, of which 16 were waited for; matrix products, arithmetic and copies ran while one was open for 6% of the time, Pallas kernels for 0%

profile of v1, /device:TPU:0, one launch (start us, length us, event | category | flops | bytes accessed | tf_op | source)
XLA Modules:
  0.0 168.1 jit_solution(360631112694692889)
XLA Ops:
  0.6 4.4 %all-to-all-start = ((bf16[2,80,512]{2,1,0:T(8,128)(2,1)}), bf16[2,80,512]{2,1,0:T(8,128)(2,1)S(1)}, u32[]{:S(2)}, u32[]{:S(2)}) async-start(bf16[2,80,512]{2,1,0:T(8,128)(2,1)} %bitcast.129), calls=%async_computation | async-start | bytes 327680 | tf_op jit(solution)/shard_map/all_to_all | solution.py:74
  6.4 3.2 %sort.17 = (s32[160]{0:T(256)}, s32[160]{0:T(256)S(1)}) sort(s32[160]{0:T(256)S(1)} %get-tuple-element.34, s32[160]{0:T(256)S(1)} %iota.46), dimensions={0}, to_apply=%region_0.1 | sort | flops 1280 | bytes 2560 | tf_op jit(solution)/shard_map/jit(argsort)/sort | solution.py:47
  12.3 13.9 %all-reduce.1 = (s32[1280]{0:T(1024)S(1)}, s32[]{:T(128)}) all-reduce(s32[1280]{0:T(1024)S(1)} %dynamic-slice_dynamic-update-slice_fusion, s32[]{:T(128)} %get-tuple-element.33), channel_id=1, replica_groups=mesh['dp'=16,'mp'=2] {'dp'}, use_global_device_ids=true, to_apply=%add | all-reduce | flops 1281 | bytes 10248
  26.2 1.3 gather_fusion
  28.5 5.6 %all-gather = bf16[128,1024]{1,0:T(8,128)(2,1)S(1)} all-gather(bf16[128,512]{1,0:T(8,128)(2,1)S(1)} %gather_fusion.1), channel_id=2, replica_groups=mesh['dp'=16,'mp'=2] {'mp'}, dimensions={1}, use_global_device_ids=true | all-gather | bytes 393216 | tf_op jit(solution)/shard_map/all_gather | solution.py:73
  34.4 7.2 %collective-permute-done = bf16[80,1024]{1,0:T(8,128)(2,1)S(1)} collective-permute-done((bf16[80,1024]{1,0:T(8,128)(2,1)S(1)}, bf16[80,1024]{1,0:T(8,128)(2,1)S(1)}, u32[]{:S(2)}, u32[]{:S(2)}) %collective-permute-start) | collective-permute-done | bytes 163872 | tf_op jit(solution)/shard_map/ppermute | solution.py:82
  41.8 7.2 %collective-permute-done.1 = bf16[80,1024]{1,0:T(8,128)(2,1)S(1)} collective-permute-done((bf16[80,1024]{1,0:T(8,128)(2,1)S(1)}, bf16[80,1024]{1,0:T(8,128)(2,1)S(1)}, u32[]{:S(2)}, u32[]{:S(2)}) %collective-permute-start.1) | collective-permute-done | bytes 163872 | tf_op jit(solution)/shard_map/ppermute | solution.py:82
  49.3 7.2 %collective-permute-done.2 = bf16[80,1024]{1,0:T(8,128)(2,1)S(1)} collective-permute-done((bf16[80,1024]{1,0:T(8,128)(2,1)S(1)}, bf16[80,1024]{1,0:T(8,128)(2,1)S(1)}, u32[]{:S(2)}, u32[]{:S(2)}) %collective-permute-start.2) | collective-permute-done | bytes 163872 | tf_op jit(solution)/shard_map/ppermute | solution.py:82
  56.7 7.2 %collective-permute-done.3 = bf16[80,1024]{1,0:T(8,128)(2,1)S(1)} collective-permute-done((bf16[80,1024]{1,0:T(8,128)(2,1)S(1)}, bf16[80,1024]{1,0:T(8,128)(2,1)S(1)}, u32[]{:S(2)}, u32[]{:S(2)}) %collective-permute-start.3) | collective-permute-done | bytes 163872 | tf_op jit(solution)/shard_map/ppermute | solution.py:82
  64.1 7.2 %collective-permute-done.4 = bf16[80,1024]{1,0:T(8,128)(2,1)S(1)} collective-permute-done((bf16[80,1024]{1,0:T(8,128)(2,1)S(1)}, bf16[80,1024]{1,0:T(8,128)(2,1)S(1)}, u32[]{:S(2)}, u32[]{:S(2)}) %collective-permute-start.4) | collective-permute-done | bytes 163872 | tf_op jit(solution)/shard_map/ppermute | solution.py:82
  71.6 7.2 %collective-permute-done.5 = bf16[80,1024]{1,0:T(8,128)(2,1)S(1)} collective-permute-done((bf16[80,1024]{1,0:T(8,128)(2,1)S(1)}, bf16[80,1024]{1,0:T(8,128)(2,1)S(1)}, u32[]{:S(2)}, u32[]{:S(2)}) %collective-permute-start.5) | collective-permute-done | bytes 163872 | tf_op jit(solution)/shard_map/ppermute | solution.py:82
  79.0 7.2 %collective-permute-done.6 = bf16[80,1024]{1,0:T(8,128)(2,1)S(1)} collective-permute-done((bf16[80,1024]{1,0:T(8,128)(2,1)S(1)}, bf16[80,1024]{1,0:T(8,128)(2,1)S(1)}, u32[]{:S(2)}, u32[]{:S(2)}) %collective-permute-start.6) | collective-permute-done | bytes 163872 | tf_op jit(solution)/shard_map/ppermute | solution.py:82
  86.5 7.2 %collective-permute-done.7 = bf16[80,1024]{1,0:T(8,128)(2,1)S(1)} collective-permute-done((bf16[80,1024]{1,0:T(8,128)(2,1)S(1)}, bf16[80,1024]{1,0:T(8,128)(2,1)S(1)}, u32[]{:S(2)}, u32[]{:S(2)}) %collective-permute-start.7) | collective-permute-done | bytes 163872 | tf_op jit(solution)/shard_map/ppermute | solution.py:82
  93.9 7.2 %collective-permute-done.8 = bf16[80,1024]{1,0:T(8,128)(2,1)S(1)} collective-permute-done((bf16[80,1024]{1,0:T(8,128)(2,1)S(1)}, bf16[80,1024]{1,0:T(8,128)(2,1)S(1)}, u32[]{:S(2)}, u32[]{:S(2)}) %collective-permute-start.8) | collective-permute-done | bytes 163872 | tf_op jit(solution)/shard_map/ppermute | solution.py:82
  101.4 7.2 %collective-permute-done.9 = bf16[80,1024]{1,0:T(8,128)(2,1)S(1)} collective-permute-done((bf16[80,1024]{1,0:T(8,128)(2,1)S(1)}, bf16[80,1024]{1,0:T(8,128)(2,1)S(1)}, u32[]{:S(2)}, u32[]{:S(2)}) %collective-permute-start.9) | collective-permute-done | bytes 163872 | tf_op jit(solution)/shard_map/ppermute | solution.py:82
  108.8 7.2 %collective-permute-done.10 = bf16[80,1024]{1,0:T(8,128)(2,1)S(1)} collective-permute-done((bf16[80,1024]{1,0:T(8,128)(2,1)S(1)}, bf16[80,1024]{1,0:T(8,128)(2,1)S(1)}, u32[]{:S(2)}, u32[]{:S(2)}) %collective-permute-start.10) | collective-permute-done | bytes 163872 | tf_op jit(solution)/shard_map/ppermute | solution.py:82
  116.2 7.2 %collective-permute-done.11 = bf16[80,1024]{1,0:T(8,128)(2,1)S(1)} collective-permute-done((bf16[80,1024]{1,0:T(8,128)(2,1)S(1)}, bf16[80,1024]{1,0:T(8,128)(2,1)S(1)}, u32[]{:S(2)}, u32[]{:S(2)}) %collective-permute-start.11) | collective-permute-done | bytes 163872 | tf_op jit(solution)/shard_map/ppermute | solution.py:82
  123.7 7.2 %collective-permute-done.12 = bf16[80,1024]{1,0:T(8,128)(2,1)S(1)} collective-permute-done((bf16[80,1024]{1,0:T(8,128)(2,1)S(1)}, bf16[80,1024]{1,0:T(8,128)(2,1)S(1)}, u32[]{:S(2)}, u32[]{:S(2)}) %collective-permute-start.12) | collective-permute-done | bytes 163872 | tf_op jit(solution)/shard_map/ppermute | solution.py:82
  131.1 7.2 %collective-permute-done.13 = bf16[80,1024]{1,0:T(8,128)(2,1)S(1)} collective-permute-done((bf16[80,1024]{1,0:T(8,128)(2,1)S(1)}, bf16[80,1024]{1,0:T(8,128)(2,1)S(1)}, u32[]{:S(2)}, u32[]{:S(2)}) %collective-permute-start.13) | collective-permute-done | bytes 163872 | tf_op jit(solution)/shard_map/ppermute | solution.py:82
  138.6 7.2 %collective-permute-done.14 = bf16[80,1024]{1,0:T(8,128)(2,1)S(1)} collective-permute-done((bf16[80,1024]{1,0:T(8,128)(2,1)S(1)}, bf16[80,1024]{1,0:T(8,128)(2,1)S(1)}, u32[]{:S(2)}, u32[]{:S(2)}) %collective-permute-start.14) | collective-permute-done | bytes 163872 | tf_op jit(solution)/shard_map/ppermute | solution.py:82
  148.0 4.2 %all-gather.3 = f32[2,1,128]{2,1,0:T(1,128)S(1)} all-gather(f32[1,1,128]{2,1,0:T(1,128)S(1)} %bitcast.131), channel_id=3, replica_groups=mesh['dp'=16,'mp'=2] {'mp'}, dimensions={0}, use_global_device_ids=true | all-gather | bytes 1536 | tf_op jit(solution)/shard_map/all_gather | solution.py:17
  152.2 4.2 %all-gather.4 = f32[2,1,128]{2,1,0:T(1,128)S(1)} all-gather(f32[1,1,128]{2,1,0:T(1,128)S(1)} %bitcast.130), channel_id=4, replica_groups=mesh['dp'=16,'mp'=2] {'mp'}, dimensions={0}, use_global_device_ids=true | all-gather | bytes 1536 | tf_op jit(solution)/shard_map/all_gather | solution.py:17
  157.6 3.5 %all-to-all-start.1 = ((f32[16,1,80]{2,1,0:T(1,128)}), f32[16,1,80]{2,1,0:T(1,128)S(1)}, u32[]{:S(2)}, u32[]{:S(2)}) async-start(f32[16,1,80]{2,1,0:T(1,128)} %bitcast.25), calls=%async_computation.1 | async-start | bytes 16384 | tf_op jit(solution)/shard_map/all_to_all | solution.py:94
  161.8 5.7 %all-to-all-done.1 = f32[16,1,80]{2,1,0:T(1,128)S(1)} async-done(((f32[16,1,80]{2,1,0:T(1,128)}), f32[16,1,80]{2,1,0:T(1,128)S(1)}, u32[]{:S(2)}, u32[]{:S(2)}) %all-to-all-start.1) | async-done | bytes 5152 | tf_op jit(solution)/shard_map/all_to_all | solution.py:94
  (63 shorter events, 12.3 us)
Async XLA Ops:
  0.6 26.9 %copy-start = (bf16[160,512]{1,0:T(8,128)(2,1)S(1)}, bf16[160,512]{1,0:T(8,128)(2,1)}, u32[]{:S(2)}) copy-start(bf16[160,512]{1,0:T(8,128)(2,1)} %param.4) | copy-start | bytes 491524
  0.6 33.4 %all-to-all-start = ((bf16[2,80,512]{2,1,0:T(8,128)(2,1)}), bf16[2,80,512]{2,1,0:T(8,128)(2,1)S(1)}, u32[]{:S(2)}, u32[]{:S(2)}) async-start(bf16[2,80,512]{2,1,0:T(8,128)(2,1)} %bitcast.129), calls=%async_computation | async-start | bytes 327680 | tf_op jit(solution)/shard_map/all_to_all | solution.py:74
  5.1 0.7 copy-start.1
  9.6 0.7 copy-start.3
  11.5 0.7 copy-start.2
  34.1 7.5 %collective-permute-start = (bf16[80,1024]{1,0:T(8,128)(2,1)S(1)}, bf16[80,1024]{1,0:T(8,128)(2,1)S(1)}, u32[]{:S(2)}, u32[]{:S(2)}) collective-permute-start(bf16[80,1024]{1,0:T(8,128)(2,1)S(1)} %bitcast.126), channel_id=1, source_target_pairs={{0,2},{2,4},{4,6},{6,8},{8,10},{10,12},{12,14},{14,16},{16,18},{18... | collective-permute-start | bytes 491528 | tf_op jit(solution)/shard_map/ppermute | solution.py:82
  41.6 7.4 %collective-permute-start.1 = (bf16[80,1024]{1,0:T(8,128)(2,1)S(1)}, bf16[80,1024]{1,0:T(8,128)(2,1)S(1)}, u32[]{:S(2)}, u32[]{:S(2)}) collective-permute-start(bf16[80,1024]{1,0:T(8,128)(2,1)S(1)} %collective-permute-done), channel_id=1, source_target_pairs={{0,2},{2,4},{4,6},{6,8},{8,10},{10,12},{12,14},{14,16},{16,18},{18... | collective-permute-start | bytes 491528 | tf_op jit(solution)/shard_map/ppermute | solution.py:82
  49.0 7.4 %collective-permute-start.2 = (bf16[80,1024]{1,0:T(8,128)(2,1)S(1)}, bf16[80,1024]{1,0:T(8,128)(2,1)S(1)}, u32[]{:S(2)}, u32[]{:S(2)}) collective-permute-start(bf16[80,1024]{1,0:T(8,128)(2,1)S(1)} %collective-permute-done.1), channel_id=1, source_target_pairs={{0,2},{2,4},{4,6},{6,8},{8,10},{10,12},{12,14},{14,16},{16,18},{18... | collective-permute-start | bytes 491528 | tf_op jit(solution)/shard_map/ppermute | solution.py:82
  56.5 7.4 %collective-permute-start.3 = (bf16[80,1024]{1,0:T(8,128)(2,1)S(1)}, bf16[80,1024]{1,0:T(8,128)(2,1)S(1)}, u32[]{:S(2)}, u32[]{:S(2)}) collective-permute-start(bf16[80,1024]{1,0:T(8,128)(2,1)S(1)} %collective-permute-done.2), channel_id=1, source_target_pairs={{0,2},{2,4},{4,6},{6,8},{8,10},{10,12},{12,14},{14,16},{16,18},{18... | collective-permute-start | bytes 491528 | tf_op jit(solution)/shard_map/ppermute | solution.py:82
  63.9 7.4 %collective-permute-start.4 = (bf16[80,1024]{1,0:T(8,128)(2,1)S(1)}, bf16[80,1024]{1,0:T(8,128)(2,1)S(1)}, u32[]{:S(2)}, u32[]{:S(2)}) collective-permute-start(bf16[80,1024]{1,0:T(8,128)(2,1)S(1)} %collective-permute-done.3), channel_id=1, source_target_pairs={{0,2},{2,4},{4,6},{6,8},{8,10},{10,12},{12,14},{14,16},{16,18},{18... | collective-permute-start | bytes 491528 | tf_op jit(solution)/shard_map/ppermute | solution.py:82
  71.4 7.4 %collective-permute-start.5 = (bf16[80,1024]{1,0:T(8,128)(2,1)S(1)}, bf16[80,1024]{1,0:T(8,128)(2,1)S(1)}, u32[]{:S(2)}, u32[]{:S(2)}) collective-permute-start(bf16[80,1024]{1,0:T(8,128)(2,1)S(1)} %collective-permute-done.4), channel_id=1, source_target_pairs={{0,2},{2,4},{4,6},{6,8},{8,10},{10,12},{12,14},{14,16},{16,18},{18... | collective-permute-start | bytes 491528 | tf_op jit(solution)/shard_map/ppermute | solution.py:82
  78.8 7.4 %collective-permute-start.6 = (bf16[80,1024]{1,0:T(8,128)(2,1)S(1)}, bf16[80,1024]{1,0:T(8,128)(2,1)S(1)}, u32[]{:S(2)}, u32[]{:S(2)}) collective-permute-start(bf16[80,1024]{1,0:T(8,128)(2,1)S(1)} %collective-permute-done.5), channel_id=1, source_target_pairs={{0,2},{2,4},{4,6},{6,8},{8,10},{10,12},{12,14},{14,16},{16,18},{18... | collective-permute-start | bytes 491528 | tf_op jit(solution)/shard_map/ppermute | solution.py:82
  86.2 7.4 %collective-permute-start.7 = (bf16[80,1024]{1,0:T(8,128)(2,1)S(1)}, bf16[80,1024]{1,0:T(8,128)(2,1)S(1)}, u32[]{:S(2)}, u32[]{:S(2)}) collective-permute-start(bf16[80,1024]{1,0:T(8,128)(2,1)S(1)} %collective-permute-done.6), channel_id=1, source_target_pairs={{0,2},{2,4},{4,6},{6,8},{8,10},{10,12},{12,14},{14,16},{16,18},{18... | collective-permute-start | bytes 491528 | tf_op jit(solution)/shard_map/ppermute | solution.py:82
  93.7 7.4 %collective-permute-start.8 = (bf16[80,1024]{1,0:T(8,128)(2,1)S(1)}, bf16[80,1024]{1,0:T(8,128)(2,1)S(1)}, u32[]{:S(2)}, u32[]{:S(2)}) collective-permute-start(bf16[80,1024]{1,0:T(8,128)(2,1)S(1)} %collective-permute-done.7), channel_id=1, source_target_pairs={{0,2},{2,4},{4,6},{6,8},{8,10},{10,12},{12,14},{14,16},{16,18},{18... | collective-permute-start | bytes 491528 | tf_op jit(solution)/shard_map/ppermute | solution.py:82
  101.1 7.4 %collective-permute-start.9 = (bf16[80,1024]{1,0:T(8,128)(2,1)S(1)}, bf16[80,1024]{1,0:T(8,128)(2,1)S(1)}, u32[]{:S(2)}, u32[]{:S(2)}) collective-permute-start(bf16[80,1024]{1,0:T(8,128)(2,1)S(1)} %collective-permute-done.8), channel_id=1, source_target_pairs={{0,2},{2,4},{4,6},{6,8},{8,10},{10,12},{12,14},{14,16},{16,18},{18... | collective-permute-start | bytes 491528 | tf_op jit(solution)/shard_map/ppermute | solution.py:82
  108.6 7.4 %collective-permute-start.10 = (bf16[80,1024]{1,0:T(8,128)(2,1)S(1)}, bf16[80,1024]{1,0:T(8,128)(2,1)S(1)}, u32[]{:S(2)}, u32[]{:S(2)}) collective-permute-start(bf16[80,1024]{1,0:T(8,128)(2,1)S(1)} %collective-permute-done.9), channel_id=1, source_target_pairs={{0,2},{2,4},{4,6},{6,8},{8,10},{10,12},{12,14},{14,16},{16,18},{18... | collective-permute-start | bytes 491528 | tf_op jit(solution)/shard_map/ppermute | solution.py:82
  116.0 7.4 %collective-permute-start.11 = (bf16[80,1024]{1,0:T(8,128)(2,1)S(1)}, bf16[80,1024]{1,0:T(8,128)(2,1)S(1)}, u32[]{:S(2)}, u32[]{:S(2)}) collective-permute-start(bf16[80,1024]{1,0:T(8,128)(2,1)S(1)} %collective-permute-done.10), channel_id=1, source_target_pairs={{0,2},{2,4},{4,6},{6,8},{8,10},{10,12},{12,14},{14,16},{16,18},{18... | collective-permute-start | bytes 491528 | tf_op jit(solution)/shard_map/ppermute | solution.py:82
  123.5 7.4 %collective-permute-start.12 = (bf16[80,1024]{1,0:T(8,128)(2,1)S(1)}, bf16[80,1024]{1,0:T(8,128)(2,1)S(1)}, u32[]{:S(2)}, u32[]{:S(2)}) collective-permute-start(bf16[80,1024]{1,0:T(8,128)(2,1)S(1)} %collective-permute-done.11), channel_id=1, source_target_pairs={{0,2},{2,4},{4,6},{6,8},{8,10},{10,12},{12,14},{14,16},{16,18},{18... | collective-permute-start | bytes 491528 | tf_op jit(solution)/shard_map/ppermute | solution.py:82
  130.9 7.4 %collective-permute-start.13 = (bf16[80,1024]{1,0:T(8,128)(2,1)S(1)}, bf16[80,1024]{1,0:T(8,128)(2,1)S(1)}, u32[]{:S(2)}, u32[]{:S(2)}) collective-permute-start(bf16[80,1024]{1,0:T(8,128)(2,1)S(1)} %collective-permute-done.12), channel_id=1, source_target_pairs={{0,2},{2,4},{4,6},{6,8},{8,10},{10,12},{12,14},{14,16},{16,18},{18... | collective-permute-start | bytes 491528 | tf_op jit(solution)/shard_map/ppermute | solution.py:82
  138.3 7.4 %collective-permute-start.14 = (bf16[80,1024]{1,0:T(8,128)(2,1)S(1)}, bf16[80,1024]{1,0:T(8,128)(2,1)S(1)}, u32[]{:S(2)}, u32[]{:S(2)}) collective-permute-start(bf16[80,1024]{1,0:T(8,128)(2,1)S(1)} %collective-permute-done.13), channel_id=1, source_target_pairs={{0,2},{2,4},{4,6},{6,8},{8,10},{10,12},{12,14},{14,16},{16,18},{18... | collective-permute-start | bytes 491528 | tf_op jit(solution)/shard_map/ppermute | solution.py:82
  157.6 9.9 %all-to-all-start.1 = ((f32[16,1,80]{2,1,0:T(1,128)}), f32[16,1,80]{2,1,0:T(1,128)S(1)}, u32[]{:S(2)}, u32[]{:S(2)}) async-start(f32[16,1,80]{2,1,0:T(1,128)} %bitcast.25), calls=%async_computation.1 | async-start | bytes 16384 | tf_op jit(solution)/shard_map/all_to_all | solution.py:94
